TPU v7x, 16 devices: a 4x2x1 block of a 4x4x8 slice. The times are simulated.
16 devices in a mesh: dp: 2 (over y, z), ep: 8 (over x, core).
Axes of the slice: x: 4, y: 2, z: 1, core: 2. Of those that a mesh axis runs over, the one named last changes fastest.
The devices are a block of a 4x4x8 slice.
Arguments:
- x: bfloat16 [2, 8, 384, 2048], P('dp', 'ep'), parts along dimension 0
- expert: int32 [2, 8, 384, 6], P('dp', 'ep'), parts along dimension 0
- slot: int32 [2, 8, 384, 6], P('dp', 'ep'), parts along dimension 0
- gate: float32 [2, 8, 384, 6], P('dp', 'ep'), parts along dimension 0
- w_gate: bfloat16 [64, 2048, 1408], P('ep')
- w_up: bfloat16 [64, 2048, 1408], P('ep')
- w_down: bfloat16 [64, 1408, 2048], P('ep')
- s_gate: bfloat16 [2048, 2816], replicated
- s_up: bfloat16 [2048, 2816], replicated
- s_down: bfloat16 [2816, 2048], replicated
Outputs:
- y: bfloat16 [2, 8, 384, 2048], P('dp', 'ep'), parts along dimension 0
There are 2 independent parts. A program takes and returns all parts, laid end to end along the dimension named above; an argument that names none is the same for every part.
All inputs are finite; a program needn't handle non-finite values.
Results may differ from a plain program's by a relative error of at most 0.009.
Values are sent between devices in bfloat16 or wider.
A program may use at most 768 MiB of HBM per device.

v0:
```python
import jax
import jax.numpy as jnp
from jax import lax
from jax.sharding import NamedSharding, PartitionSpec as P


def einsum(form, a, b):
    return jnp.einsum(form, a.astype(jnp.float32), b.astype(jnp.float32))


def for_all(x, s_gate, s_up, s_down):
    h = jax.nn.silu(einsum("...d,df->...f", x, s_gate)) * einsum("...d,df->...f", x, s_up)
    return einsum("...f,fd->...d", h.astype(jnp.bfloat16), s_down)


def solution(mesh):
    def placed(v, *spec):
        return lax.with_sharding_constraint(v, NamedSharding(mesh, P(*spec)))

    def step(x, expert, slot, gate, w_gate, w_up, w_down, s_gate, s_up, s_down):
        experts, (tokens, top) = w_gate.shape[0], expert.shape[2:]
        slots = 5 * tokens * top // (4 * experts)
        to_expert = jax.nn.one_hot(expert, experts, dtype=jnp.bfloat16)
        to_slot = jax.nn.one_hot(slot, slots, dtype=jnp.bfloat16)
        weighted = to_expert * gate[..., None].astype(jnp.bfloat16)
        dispatch = einsum("abtke,abtkc->abtec", to_expert, to_slot).astype(jnp.bfloat16)
        combine = einsum("abtke,abtkc->abtec", weighted, to_slot).astype(jnp.bfloat16)
        z = einsum("abtec,abtd->aebcd", dispatch, x).astype(jnp.bfloat16)
        z = placed(z, "dp", None, "ep", None, None)
        z = placed(z, "dp", "ep", None, None, None)
        h = jax.nn.silu(einsum("aebcd,edf->aebcf", z, w_gate))
        h = (h * einsum("aebcd,edf->aebcf", z, w_up)).astype(jnp.bfloat16)
        out = einsum("aebcf,efd->aebcd", h, w_down).astype(jnp.bfloat16)
        out = placed(out, "dp", "ep", None, None, None)
        out = placed(out, "dp", None, "ep", None, None)
        y = einsum("abtec,aebcd->abtd", combine, out)
        return (y + for_all(x, s_gate, s_up, s_down)).astype(jnp.bfloat16)

    return step
```

profile of v0, /device:TPU:112, one launch (start us, length us, event | category | flops | bytes accessed | tf_op | source)
XLA Modules:
  0.0 447.4 jit_solution(1717721862677202285)
XLA Ops:
  0.0 0.0 copy-start
  0.0 0.9 copy.21
  1.0 0.8 copy.23
  1.8 4.2 convolution_convert_fusion
  6.0 0.0 copy-done
  6.0 6.9 %convert_bitcast_fusion.1 = bf16[1,8,8,1,45,2048]{5,2,1,4,3,0:T(8,128)(2,1)S(1)} fusion(bf16[384,64,45]{1,2,0:T(8,128)(2,1)S(1)} %convolution_convert_fusion, bf16[1,1,384,2048]{3,2,1,0:T(8,128)(2,1)S(1)} %copy-done), kind=kOutput, calls=%fused_computation.19 | convolution fusion | flops 4535746560 | bytes 15581184 | tf_op jit(solution)/abtec,abtd->aebcd/dot_general | solution.py:8
  12.9 1.4 copy.13
  14.3 136.3 %all-to-all.4 = bf16[1,8,8,1,45,2048]{5,2,4,3,0,1:T(8,128)(2,1)} all-to-all(bf16[1,8,8,1,45,2048]{5,2,4,3,0,1:T(8,128)(2,1)S(1)} %copy.13), channel_id=1, replica_groups=mesh['dp'=2,'ep'=8] {'ep'}, dimensions={1} | all-to-all | bytes 23592960 | tf_op jit(solution)/sharding_constraint;jit(solution)/sharding_constraint | solution.py:18
  150.6 36.5 %fusion.2 = f32[8,8,45,1408]{3,2,1,0:T(8,128)} fusion(bf16[8,2048,1408]{2,1,0:T(8,128)(2,1)} %param.5, bf16[1,8,8,1,45,2048]{5,2,4,3,0,1:T(8,128)(2,1)} %all-to-all.4), kind=kOutput, calls=%fused_computation.2 | convolution fusion | flops 16609443840 | bytes 74153984 | tf_op jit(solution)/aebcd,edf->aebcf/dot_general | solution.py:8
  187.2 67.4 %fusion.6 = bf16[1,8,8,45,1408]{4,3,2,1,0:T(8,128)(2,1)} fusion(f32[8,8,45,1408]{3,2,1,0:T(8,128)} %fusion.2, bf16[8,2048,1408]{2,1,0:T(8,128)(2,1)} %param.4, bf16[1,8,8,1,45,2048]{5,2,4,3,0,1:T(8,128)(2,1)} %all-to-all.4), kind=kOutput, calls=%fused_computation.7 | convolution fusion | flops 16633774080 | bytes 82264064 | tf_op jit(solution)/aebcd,edf->aebcf/dot_general | solution.py:8
  254.6 29.3 %convert_bitcast_fusion = bf16[1,8,8,1,45,2048]{5,4,2,1,3,0:T(8,128)(2,1)} fusion(bf16[8,1408,2048]{2,1,0:T(8,128)(2,1)} %param.6, bf16[1,8,8,45,1408]{4,3,2,1,0:T(8,128)(2,1)} %fusion.6), kind=kOutput, calls=%fused_computation.15 | convolution fusion | flops 16615342080 | bytes 66043904 | tf_op jit(solution)/aebcf,efd->aebcd/dot_general | solution.py:8
  283.9 14.3 %copy.15 = bf16[1,8,8,1,45,2048]{5,1,4,3,0,2:T(8,128)(2,1)} copy(bf16[1,8,8,1,45,2048]{5,4,2,1,3,0:T(8,128)(2,1)} %convert_bitcast_fusion) | data formatting | bytes 23592960 | tf_op jit(solution)/sharding_constraint;jit(solution)/sharding_constraint | solution.py:18
  298.1 0.0 copy-start.1
  298.1 5.6 %all-to-all-start.1 = ((bf16[1,8,8,1,45,2048]{5,1,4,3,0,2:T(8,128)(2,1)}), bf16[1,8,8,1,45,2048]{5,1,4,3,0,2:T(8,128)(2,1)}, u32[]{:S(2)}, u32[]{:S(2)}) async-start(bf16[1,8,8,1,45,2048]{5,1,4,3,0,2:T(8,128)(2,1)} %copy.15), calls=%async_computation.1 | async-start | bytes 23592960 | tf_op jit(solution)/sharding_constraint;jit(solution)/sharding_constraint | solution.py:18
  303.7 0.0 copy-done.1
  303.8 0.2 copy.22
  304.0 5.6 %convolution_convert_fusion.1 = bf16[384,64,45]{1,2,0:T(8,128)(2,1)} fusion(s32[384,6]{1,0:T(8,128)S(1)} %bitcast.115, s32[384,6]{1,0:T(8,128)S(1)} %bitcast.113, bf16[384,6]{1,0:T(8,128)(2,1)S(1)} %bitcast.116), kind=kOutput, calls=%fused_computation.33 | convolution fusion | flops 14775552 | bytes 2234880 | tf_op jit(solution)/abtke,abtkc->abtec/dot_general | solution.py:8
  309.6 9.4 %convolution_bitcast_fusion.1 = f32[1,1,384,2816]{3,2,1,0:T(8,128)} fusion(bf16[2048,2816]{1,0:T(8,128)(2,1)} %param.7, bf16[1,1,384,2048]{3,2,1,0:T(8,128)(2,1)S(1)} %copy-done), kind=kOutput, calls=%fused_computation.25 | convolution fusion | flops 4429185024 | bytes 17432576 | tf_op jit(solution)/...d,df->...f/dot_general | solution.py:8
  319.0 19.7 %fusion.49 = f32[384,2048]{1,0:T(8,128)} fusion(bf16[2816,2048]{1,0:T(8,128)(2,1)} %param.9, bf16[2048,2816]{1,0:T(8,128)(2,1)} %param.8, f32[1,1,384,2816]{3,2,1,0:T(8,128)} %convolution_bitcast_fusion.1, bf16[1,1,384,2048]{3,2,1,0:T(8,128)(2,1)S(1)} %copy-done), kind=kOutput, calls=%fused_computation.43 | convolution fusion | flops 8864858112 | bytes 32112640 | tf_op jit(solution)/...f,fd->...d/dot_general | solution.py:8
  338.7 95.9 %all-to-all-done.1 = bf16[1,8,8,1,45,2048]{5,1,4,3,0,2:T(8,128)(2,1)} async-done(((bf16[1,8,8,1,45,2048]{5,1,4,3,0,2:T(8,128)(2,1)}), bf16[1,8,8,1,45,2048]{5,1,4,3,0,2:T(8,128)(2,1)}, u32[]{:S(2)}, u32[]{:S(2)}) %all-to-all-start.1) | async-done | bytes 11796512 | tf_op jit(solution)/sharding_constraint;jit(solution)/sharding_constraint | solution.py:18
  434.6 12.3 %fusion.34 = bf16[1,1,384,2048]{3,2,1,0:T(8,128)(2,1)} fusion(f32[384,2048]{1,0:T(8,128)} %fusion.49, bf16[1,8,8,1,45,2048]{5,1,4,3,0,2:T(8,128)(2,1)} %all-to-all-done.1, bf16[384,64,45]{1,2,0:T(8,128)(2,1)} %convolution_convert_fusion.1), kind=kOutput, calls=%fused_computation.34 | convolution fusion | flops 4531421184 | bytes 18726912 | tf_op jit(solution)/abtec,aebcd->abtd/dot_general | solution.py:8
  (1 shorter events, 0.0 us)
Async XLA Ops:
  0.0 6.0 %copy-start = (bf16[1,1,384,2048]{3,2,1,0:T(8,128)(2,1)S(1)}, bf16[1,1,384,2048]{3,2,1,0:T(8,128)(2,1)}, u32[]{:S(2)}) copy-start(bf16[1,1,384,2048]{3,2,1,0:T(8,128)(2,1)} %param.3) | copy-start | bytes 4718596
  298.1 5.6 %copy-start.1 = (f32[1,1,384,6]{2,1,3,0:T(1,128)S(1)}, f32[1,1,384,6]{2,1,3,0:T(1,128)}, u32[]{:S(2)}) copy-start(f32[1,1,384,6]{2,1,3,0:T(1,128)} %param.1) | copy-start | bytes 27652
  298.1 136.5 %all-to-all-start.1 = ((bf16[1,8,8,1,45,2048]{5,1,4,3,0,2:T(8,128)(2,1)}), bf16[1,8,8,1,45,2048]{5,1,4,3,0,2:T(8,128)(2,1)}, u32[]{:S(2)}, u32[]{:S(2)}) async-start(bf16[1,8,8,1,45,2048]{5,1,4,3,0,2:T(8,128)(2,1)} %copy.15), calls=%async_computation.1 | async-start | bytes 23592960 | tf_op jit(solution)/sharding_constraint;jit(solution)/sharding_constraint | solution.py:18
where the time goes:
time: 455 us; the launch traced here: 447 us
  matrix products  191 us (42%)
  blocking collectives  136 us (30%)
  waiting for transfers between devices  95.9 us (21%)
  local copies, waits for them, and re-layouts  17.7 us (4%)
  starting transfers between devices  5.59 us (1%)
    dot_general x9, matrix products, einsum(): return jnp.einsum(form, a.astype(jnp.float32), b.astype(jnp.float32))  191 us
    another operation x1, blocking collectives, placed(): return lax.with_sharding_constraint(v, NamedSharding(mesh, P(*spec)))  136 us
    another operation x1, waiting for transfers between devices, placed(): return lax.with_sharding_constraint(v, NamedSharding(mesh, P(*spec)))  95.9 us
    another operation x2, local copies, waits for them, and re-layouts, placed(): return lax.with_sharding_constraint(v, NamedSharding(mesh, P(*spec)))  15.7 us
  transfers between devices with their start and end apart: 1, of which 1 were waited for; matrix products, arithmetic and copies ran while one was open for 8% of the time, Pallas kernels for 0%

commit v1 on v0

v1 whole, which is shorter than its diff:
```python
import jax
import jax.numpy as jnp
from jax import lax
from jax.sharding import PartitionSpec as P

F32, BF16 = jnp.float32, jnp.bfloat16


def dot(form, a, b):
    return jnp.einsum(form, a, b, preferred_element_type=F32)


def solution(mesh):
    def body(x, expert, slot, gate, w_gate, w_up, w_down, s_gate, s_up, s_down):
        x, expert, slot, gate = x[0, 0], expert[0, 0], slot[0, 0], gate[0, 0]
        tokens, top = expert.shape
        mine = w_gate.shape[0]
        slots = 5 * tokens * top // (4 * mine * mesh.shape["ep"])
        place = jnp.where(slot < slots, expert * slots + slot, -1)
        xs = lax.all_gather(x, "ep")
        places = lax.all_gather(place, "ep")
        gates = lax.all_gather(gate, "ep")
        at = places - lax.axis_index("ep") * (mine * slots)
        hot = (at[..., None] == lax.broadcasted_iota(jnp.int32, (1, 1, 1, mine * slots), 3))
        dispatch = jnp.any(hot, axis=2).astype(BF16)
        combine = jnp.sum(jnp.where(hot, gates[..., None], 0), axis=2).astype(BF16)
        z = dot("atr,atd->ard", dispatch, xs).astype(BF16)
        z = z.reshape(z.shape[0], mine, slots, -1).swapaxes(0, 1).reshape(mine, -1, z.shape[-1])
        h = jax.nn.silu(dot("erd,edf->erf", z, w_gate)) * dot("erd,edf->erf", z, w_up)
        out = dot("erf,efd->erd", h.astype(BF16), w_down).astype(BF16)
        out = out.reshape(mine, -1, slots, out.shape[-1]).swapaxes(0, 1).reshape(xs.shape[0], mine * slots, -1)
        y = dot("atr,ard->atd", combine, out).astype(BF16)
        y = lax.psum_scatter(y, "ep")
        hs = jax.nn.silu(dot("td,df->tf", x, s_gate)) * dot("td,df->tf", x, s_up)
        shared = dot("tf,fd->td", hs.astype(BF16), s_down)
        return (y.astype(F32) + shared).astype(BF16)[None, None]

    token, part, whole = P("dp", "ep"), P("ep"), P()
    return jax.shard_map(
        body,
        mesh=mesh,
        in_specs=(token,) * 4 + (part,) * 3 + (whole,) * 3,
        out_specs=token,
        check_vma=False,
    )
```

time: 455 us -> 451 us (level)
  blocking collectives: 136 us -> 46.2 us
  local copies, waits for them, and re-layouts: 17.7 us -> 78.3 us
  waiting for transfers between devices: 95.9 us -> 59.8 us
  matrix products: 191 us -> 220 us
  other arithmetic: 0.01 us -> 24.4 us
  between operations: 0.52 us -> 13.9 us
  starting transfers between devices: 5.59 us -> 0.06 us
    another operation x1 -> x0, blocking collectives: 136 us -> none  [placed(): return lax.with_sharding_constraint(v, NamedSharding(mesh, P(*spec)))]
    another operation x1 -> x0, waiting for transfers between devices: 95.9 us -> none  [placed(): return lax.with_sharding_constraint(v, NamedSharding(mesh, P(*spec)))]
    reduce_scatter x0 -> x1, waiting for transfers between devices: none -> 59 us  [body(): y = lax.psum_scatter(y, 'ep')]
    all_gather x0 -> x2, blocking collectives: none -> 46.2 us  [the longest x1 24.6 us: body(): places = lax.all_gather(place, 'ep')]
    convert_element_type x1 -> x2, local copies, waits for them, and re-layouts: 0.18 us -> 42 us  [the longest x1 25.2 us: body(): out = dot('erf,efd->erd', h.astype(BF16), w_down).astype(BF16)]
    transpose x0 -> x2, local copies, waits for them, and re-layouts: none -> 34.9 us  [the longest x1 17.5 us: body(): z.reshape(z.shape[0], mine, slots, -1).swapaxes(0, 1)]
    dot_general x9 -> x7, matrix products: 191 us -> 220 us  [dot(): return jnp.einsum(form, a, b, preferred_element_type=F32)]
    reduce_sum x0 -> x1, other arithmetic: none -> 16 us  [body(): combine = jnp.sum(jnp.where(hot, gates[..., None], 0), axis=2).astype(BF16)]
  transfers between devices with their start and end apart: 1 -> 2, of which waited for: 1 -> 1; matrix products, arithmetic and copies ran while one was open for 8% -> 8% of each run, Pallas kernels for 0% -> 0%
where the time goes in v1:
time: 451 us; the launch traced here: 442 us
  matrix products  220 us (49%)
  local copies, waits for them, and re-layouts  78.3 us (17%)
  waiting for transfers between devices  59.8 us (13%)
  blocking collectives  46.2 us (10%)
  other arithmetic  24.4 us (5%)
  between operations  13.9 us (3%)
    dot_general x7, matrix products, dot(): return jnp.einsum(form, a, b, preferred_element_type=F32)  220 us
    reduce_scatter x1, waiting for transfers between devices, body(): y = lax.psum_scatter(y, 'ep')  59 us
    convert_element_type x1, local copies, waits for them, and re-layouts, body(): out = dot('erf,efd->erd', h.astype(BF16), w_down).astype(BF16)  25.2 us
    all_gather x1, blocking collectives, body(): places = lax.all_gather(place, 'ep')  24.6 us
    all_gather x1, blocking collectives, body(): gates = lax.all_gather(gate, 'ep')  21.6 us
    transpose x1, local copies, waits for them, and re-layouts, body(): z.reshape(z.shape[0], mine, slots, -1).swapaxes(0, 1)  17.5 us
    transpose x1, local copies, waits for them, and re-layouts, body(): out.reshape(mine, -1, slots, out.shape[-1]).swapaxes(0, 1)  17.5 us
    convert_element_type x1, local copies, waits for them, and re-layouts, body(): z = dot('atr,atd->ard', dispatch, xs).astype(BF16)  16.8 us
  transfers between devices with their start and end apart: 2, of which 1 were waited for; matrix products, arithmetic and copies ran while one was open for 8% of the time, Pallas kernels for 0%

profile of v1, /device:TPU:112, one launch (start us, length us, event | category | flops | bytes accessed | tf_op | source)
XLA Modules:
  0.0 442.3 jit_solution(17437710025637506583)
XLA Ops:
  6.5 0.0 all-gather.5.cloned.1.call-start
  6.6 0.7 all-gather.5.cloned.1.call-update
  7.3 0.1 reduce-scatter.2.cloned.1.call-start
  7.4 0.7 compare_select_fusion
  8.1 24.6 %all-gather = s32[8,1,384,6]{2,1,3,0:T(1,128)S(1)} all-gather(s32[1,1,384,6]{2,1,3,0:T(1,128)S(1)} %compare_select_fusion), channel_id=2, replica_groups=mesh['dp'=2,'ep'=8] {'ep'}, dimensions={0}, use_global_device_ids=true | all-gather | bytes 82944 | tf_op jit(solution)/shard_map/all_gather | solution.py:21
  32.8 21.6 %all-gather.1 = f32[8,1,384,6]{2,1,3,0:T(1,128)S(1)} all-gather(f32[1,1,384,6]{2,1,3,0:T(1,128)} %param.13), channel_id=3, replica_groups=mesh['dp'=2,'ep'=8] {'ep'}, dimensions={0}, use_global_device_ids=true | all-gather | bytes 82944 | tf_op jit(solution)/shard_map/all_gather | solution.py:22
  54.4 7.6 %fusion = pred[8,384,360]{1,2,0:T(8,128)(4,1)S(1)} fusion(s32[8,384,6]{1,2,0:T(8,128)S(1)} %copy.43), kind=kLoop, calls=%fused_computation.2 | loop fusion | flops 12165120 | bytes 1179648 | tf_op jit(solution)/shard_map/reduce_or | solution.py:25
  62.0 16.0 %select_reduce_fusion = bf16[8,384,360]{1,2,0:T(8,128)(2,1)} fusion(f32[8,384,6]{1,2,0:T(8,128)S(1)} %bitcast.45, s32[8,384,6]{1,2,0:T(8,128)S(1)} %copy.43), kind=kLoop, calls=%fused_computation | loop fusion | flops 18800640 | bytes 2359296 | tf_op jit(solution)/shard_map/reduce_sum | solution.py:26
  78.1 0.0 all-gather.5.cloned.1.call-done
  78.1 11.2 %fusion.14 = bf16[8,360,2048]{2,1,0:T(8,128)(2,1)S(1)} fusion(pred[8,384,360]{1,2,0:T(8,128)(4,1)S(1)} %fusion, bf16[8,1,384,2048]{3,2,1,0:T(8,128)(2,1)} %all-gather.5.cloned.1.call-done), kind=kOutput, calls=%fused_computation.13 | convolution fusion | flops 4535746560 | bytes 25485312 | tf_op jit(solution)/shard_map/atr,atd->ard/dot_general | solution.py:10
  89.3 16.8 %copy.46 = bf16[8,360,2048]{2,0,1:T(8,128)(2,1)S(1)} copy(bf16[8,360,2048]{2,1,0:T(8,128)(2,1)S(1)} %fusion.14) | data formatting | bytes 23592960 | tf_op jit(solution)/shard_map/convert_element_type | solution.py:27
  106.2 17.5 %copy.47 = bf16[8,8,45,2048]{3,0,2,1:T(8,128)(2,1)} copy(bf16[8,8,45,2048]{3,1,2,0:T(8,128)(2,1)S(1)} %bitcast.40) | data formatting | bytes 23592960 | tf_op jit(solution)/shard_map/transpose | solution.py:28
  123.6 34.8 %fusion.5 = f32[8,360,1408]{2,1,0:T(8,128)} fusion(bf16[8,2048,1408]{2,1,0:T(8,128)(2,1)} %param.15, bf16[8,360,2048]{2,0,1:T(8,128)(2,1)} %bitcast.42), kind=kOutput, calls=%fused_computation.8 | convolution fusion | flops 16609443840 | bytes 74153984 | tf_op jit(solution)/shard_map/erd,edf->erf/dot_general | solution.py:10
  158.4 67.4 %multiply_convert_fusion = bf16[8,360,1408]{2,1,0:T(8,128)(2,1)} fusion(f32[8,360,1408]{2,1,0:T(8,128)} %fusion.5, bf16[8,2048,1408]{2,1,0:T(8,128)(2,1)} %param.14, bf16[8,360,2048]{2,0,1:T(8,128)(2,1)} %bitcast.43), kind=kOutput, calls=%fused_computation.3 | convolution fusion | flops 16633774080 | bytes 82264064 | tf_op jit(solution)/shard_map/erd,edf->erf/dot_general | solution.py:10
  225.8 28.4 %convolution_convert_fusion = bf16[8,360,2048]{2,1,0:T(8,128)(2,1)} fusion(bf16[8,360,1408]{2,1,0:T(8,128)(2,1)} %multiply_convert_fusion, bf16[8,1408,2048]{2,1,0:T(8,128)(2,1)} %param.16), kind=kOutput, calls=%fused_computation.14 | convolution fusion | flops 16615342080 | bytes 66043904 | tf_op jit(solution)/shard_map/erf,efd->erd/dot_general | solution.py:10
  254.3 25.2 %copy.50 = bf16[8,360,2048]{2,0,1:T(8,128)(2,1)S(1)} copy(bf16[8,360,2048]{2,1,0:T(8,128)(2,1)} %convolution_convert_fusion) | data formatting | bytes 23592960 | tf_op jit(solution)/shard_map/convert_element_type | solution.py:30
  279.4 0.0 copy-start
  279.5 17.5 %copy.51 = bf16[8,8,45,2048]{3,0,2,1:T(8,128)(2,1)} copy(bf16[8,8,45,2048]{3,1,2,0:T(8,128)(2,1)S(1)} %bitcast.41) | data formatting | bytes 23592960 | tf_op jit(solution)/shard_map/transpose | solution.py:31
  296.9 0.0 copy-done
  296.9 48.7 %fusion.11 = bf16[8,384,2048]{2,1,0:T(8,128)(2,1)} fusion(bf16[8,360,2048]{2,0,1:T(8,128)(2,1)} %bitcast.44, bf16[8,384,360]{1,2,0:T(8,128)(2,1)S(1)} %copy-done), kind=kOutput, calls=%fused_computation.12 | convolution fusion | flops 4536139776 | bytes 26591232 | tf_op jit(solution)/shard_map/atr,ard->atd/dot_general | solution.py:10
  345.6 0.0 copy-start.1
  345.6 0.1 reduce-scatter.2.cloned.1.call-update
  345.7 1.3 copy-done.1
  347.0 9.4 %fusion.22 = f32[384,2816]{1,0:T(8,128)} fusion(bf16[2048,2816]{1,0:T(8,128)(2,1)} %param.17, bf16[1,1,384,2048]{3,2,1,0:T(8,128)(2,1)S(1)} %copy-done.1), kind=kOutput, calls=%fused_computation.22 | convolution fusion | flops 4429185024 | bytes 17432576 | tf_op jit(solution)/shard_map/td,df->tf/dot_general | solution.py:10
  356.5 59.0 %reduce-scatter.2.cloned.1.call-done = bf16[1,384,2048]{2,1,0:T(8,128)(2,1)} async-done(((bf16[8,384,2048]{2,1,0:T(8,128)(2,1)}), bf16[1,384,2048]{2,1,0:T(8,128)(2,1)}) %reduce-scatter.2.cloned.1.call-update) | async-done | bytes 1572880 | tf_op jit(solution)/shard_map/reduce_scatter | solution.py:33
  415.5 19.6 %fusion.19 = bf16[1,1,384,2048]{3,2,1,0:T(8,128)(2,1)} fusion(bf16[2816,2048]{1,0:T(8,128)(2,1)} %param.19, bf16[1,384,2048]{2,1,0:T(8,128)(2,1)} %reduce-scatter.2.cloned.1.call-done, bf16[2048,2816]{1,0:T(8,128)(2,1)} %param.18, f32[384,2816]{1,0:T(8,128)} %fusion.22, bf16[1,1,384,2048]{3,2,1,0:T(8,128)(2,1)S(1)} %copy-done.1), kind=kOutput, calls=%fused_computation.19 | convolution fusion | flops 8867217408 | bytes 32112640 | tf_op jit(solution)/shard_map/tf,fd->td/dot_general | solution.py:10
  (3 shorter events, 0.0 us)
Async XLA Ops:
  6.5 71.5 %all-gather.5.cloned.1.call-start = ((), (), s32[]{:S(2)}) async-start(), calls=%async_computation.2 | async-start | bytes 14155776 | tf_op jit(solution)/shard_map/all_gather | solution.py:20
  7.3 408.2 %reduce-scatter.2.cloned.1.call-start = ((), (), s32[]{:S(2)}) async-start(), calls=%async_computation.1 | async-start | bytes 14155776 | tf_op jit(solution)/shard_map/reduce_scatter | solution.py:33
  279.4 17.5 %copy-start = (bf16[8,384,360]{1,2,0:T(8,128)(2,1)S(1)}, bf16[8,384,360]{1,2,0:T(8,128)(2,1)}, u32[]{:S(2)}) copy-start(bf16[8,384,360]{1,2,0:T(8,128)(2,1)} %select_reduce_fusion) | copy-start | bytes 6635524
  345.6 1.4 copy-start.1
Sparse Core Ops, SparseCore 0:
  8.9 67.0 all-gather.4
  345.8 69.6 reduce-scatter.1

commit v2 on v1

v2 whole, which is shorter than its diff:
```python
import functools

import jax
import jax.numpy as jnp
from jax import lax
from jax.experimental import pallas as pl
from jax.experimental.pallas import tpu as pltpu
from jax.sharding import PartitionSpec as P

F32, BF16 = jnp.float32, jnp.bfloat16
MESH = pl.DeviceIdType.MESH
ANY = pl.BlockSpec(memory_space=pl.ANY)
VMEM_LIMIT = 67_043_328

PIECE = 256
OUT = 256
RING = 4
DOWN_RING = 6

OWN, PARTNER, RIGHT, RIGHT_X, FAR, FAR_X, LEFT, LEFT_X = range(8)


def dot(a, b):
    return jnp.dot(a, b, preferred_element_type=F32)


def neighbours(n):
    me = lax.axis_index("ep")
    core = lax.rem(me, 2)
    chip = me // 2

    def at(slot):
        c = core if slot % 2 == 0 else 1 - core
        return 2 * lax.rem(chip + slot // 2, n // 2) + c

    return me, at


def meet(peers):
    barrier = pltpu.get_barrier_semaphore()
    for peer in peers:
        pl.semaphore_signal(barrier, inc=1, device_id={"ep": peer}, device_id_type=MESH)
    pl.semaphore_wait(barrier, len(peers))


def gather_kernel(
    n, slots, x_hbm, info_hbm, wg_hbm, wu_hbm, sg_hbm, su_hbm,
    h_hbm, cw_hbm, hs_hbm,
    xg, info, acc, z, hot, cws, hs, hstage, ring,
    load_sem, info_send, info_recv, send_sem, recv_sem, w_sem, out_sem, cw_sem, h_sem,
):
    me, at = neighbours(n)
    tokens, depth = x_hbm.shape
    experts, _, ff = wg_hbm.shape
    pieces = depth // PIECE
    pad = z.shape[1] // n
    rows = experts * pad
    half = tokens // 2
    shared_steps = 2 * pieces
    total = shared_steps + pieces * experts

    top, bottom, every = pl.ds(0, half), pl.ds(half, half), pl.ds(0, tokens)
    kinds = (
        (OWN, PARTNER, PARTNER, every),
        (OWN, LEFT, RIGHT, every),
        (OWN, RIGHT, LEFT, every),
        (LEFT, FAR, RIGHT, top),
        (RIGHT, FAR, LEFT, bottom),
        (LEFT, LEFT_X, PARTNER, every),
        (RIGHT, RIGHT_X, PARTNER, every),
        (FAR, FAR_X, PARTNER, every),
    )

    def move(kind, k):
        src, dst, to, r = kinds[kind]
        return pltpu.make_async_remote_copy(
            src_ref=xg.at[k, src, r, :],
            dst_ref=xg.at[k, dst, r, :],
            send_sem=send_sem.at[kind, k],
            recv_sem=recv_sem.at[kind, k],
            device_id={"ep": at(to)},
            device_id_type=MESH,
        )

    def opposite(slot):
        return 2 * ((n // 2 - slot // 2) % (n // 2)) + slot % 2

    def tell(slot):
        back = opposite(slot)
        return pltpu.make_async_remote_copy(
            src_ref=info.at[OWN],
            dst_ref=info.at[back],
            send_sem=info_send.at[slot],
            recv_sem=info_recv.at[back],
            device_id={"ep": at(slot)},
            device_id_type=MESH,
        )

    def load_x(k):
        return pltpu.make_async_copy(x_hbm.at[:, pl.ds(k * PIECE, PIECE)], xg.at[k, OWN], load_sem.at[k])

    load_info = pltpu.make_async_copy(info_hbm, info.at[OWN], load_sem.at[pieces])

    def fetch_shared(which, k, slot):
        w = (sg_hbm, su_hbm)[which]
        return pltpu.make_async_copy(w.at[pl.ds(k * PIECE, PIECE), :], ring.at[slot], w_sem.at[slot, 0])

    def fetch_routed(k, e, slot):
        return (
            pltpu.make_async_copy(wg_hbm.at[e, pl.ds(k * PIECE, PIECE), :], ring.at[slot, :, pl.ds(0, ff)], w_sem.at[slot, 0]),
            pltpu.make_async_copy(wu_hbm.at[e, pl.ds(k * PIECE, PIECE), :], ring.at[slot, :, pl.ds(ff, ff)], w_sem.at[slot, 1]),
        )

    def start(i):
        slot = lax.rem(i, RING)

        @pl.when(i < pieces)
        def _():
            fetch_shared(0, i, slot).start()

        @pl.when((i >= pieces) & (i < shared_steps))
        def _():
            fetch_shared(1, i - pieces, slot).start()

        @pl.when((i >= shared_steps) & (i < total))
        def _():
            j = i - shared_steps
            for c in fetch_routed(j // experts, lax.rem(j, experts), slot):
                c.start()

    def accumulate(a, left, slot, first):
        width = ring.shape[2]
        for lo in range(0, width, 256):
            cut = pl.ds(lo, min(256, width - lo))
            before = jnp.where(first, 0.0, acc[a, :, cut])
            acc[a, :, cut] = before + dot(left, ring[slot, :, cut])

    for k in range(pieces):
        load_x(k).start()
    load_info.start()
    for i in range(RING - 1):
        fetch_shared(0, i, i).start()
    meet([at(s) for s in range(1, n)])
    for k in range(pieces):
        load_x(k).wait()
        if k < 2:
            move(1, k).start()
            move(2, k).start()
        move(0, k).start()
        if k == 0:
            load_info.wait()
            for s in range(1, n):
                tell(s).start()

    def shared_step(i, _):
        slot = lax.rem(i, RING)
        start(i + RING - 1)
        fetch_shared(0, 0, slot).wait()
        k = lax.rem(i, pieces)
        accumulate(i // pieces, xg[k, OWN], slot, k == 0)
        return 0

    lax.fori_loop(0, shared_steps, shared_step, 0)

    def near(k):
        move(1, k).wait_recv()
        move(2, k).wait_recv()
        move(3, k).start()
        move(4, k).start()
        move(5, k).start()
        move(6, k).start()

        @pl.when(k + 2 < pieces)
        def _():
            move(1, k + 2).start()
            move(2, k + 2).start()

    near(0)

    width = ring.shape[2]
    for lo in range(0, width, 256):
        cut = pl.ds(lo, min(256, width - lo))
        hs[:, cut] = (jax.nn.silu(acc[0, :, cut]) * acc[1, :, cut]).astype(BF16)
    hs_out = pltpu.make_async_copy(hs, hs_hbm, out_sem)
    hs_out.start()

    base = (me * rows).astype(F32)
    row = lax.broadcasted_iota(jnp.int32, (rows, tokens), 0).astype(F32) + base
    top_k = info.shape[1] // 2

    for s in range(n):
        if s:
            tell(opposite(s)).wait_recv()
        found = jnp.zeros((rows, tokens), F32)
        for j in range(top_k):
            found = jnp.where(row == info[s, pl.ds(j, 1), :], 1.0, found)
        hot[s] = found.astype(BF16)

    def weigh(s):
        found = jnp.zeros((rows, tokens), F32)
        for j in range(top_k):
            found = jnp.where(row == info[s, pl.ds(j, 1), :], info[s, pl.ds(top_k + j, 1), :], found)
        return found.T.astype(BF16)

    def cw_out(s):
        return pltpu.make_async_copy(cws.at[lax.rem(s, 2)], cw_hbm.at[s], cw_sem.at[lax.rem(s, 2)])

    def dispatch(k):
        move(0, k).wait_recv()
        move(5, k).wait_recv()
        move(6, k).wait_recv()

        def place(s):
            got = dot(hot[s], xg[k, s]).astype(BF16)
            for e in range(experts):
                z[e, s * pad : (s + 1) * pad, :] = got[e * pad : (e + 1) * pad]

        for s in (OWN, PARTNER, RIGHT, LEFT, RIGHT_X, LEFT_X):
            place(s)
        move(3, k).wait_recv()
        move(4, k).wait_recv()
        move(7, k).start()
        place(FAR)
        move(7, k).wait_recv()
        place(FAR_X)

    def piece(k, _):
        dispatch(k)

        def step(e, _):
            i = shared_steps + k * experts + e
            slot = lax.rem(i, RING)
            start(i + RING - 1)
            for c in fetch_routed(0, 0, slot):
                c.wait()
            accumulate(e, z[e], slot, k == 0)

            @pl.when(e == experts // 2 - 1)
            def _():
                near(k + 1)

            return 0

        lax.fori_loop(0, experts, step, 0)

        @pl.when(k >= 2)
        def _():
            cw_out(k - 2).wait()

        cws[lax.rem(k, 2)] = weigh(k)
        cw_out(k).start()
        return 0

    assert pieces == n
    lax.fori_loop(0, pieces - 1, piece, 0)
    last = pieces - 1
    dispatch(last)

    def h_out(e):
        return pltpu.make_async_copy(hstage.at[lax.rem(e, 2)], h_hbm.at[e], h_sem.at[lax.rem(e, 2)])

    def final_step(e, _):
        i = shared_steps + last * experts + e
        slot = lax.rem(i, RING)
        start(i + RING - 1)
        for c in fetch_routed(0, 0, slot):
            c.wait()

        @pl.when(e >= 2)
        def _():
            h_out(e - 2).wait()

        for lo in range(0, ff, 256):
            size = min(256, ff - lo)
            a, b = pl.ds(lo, size), pl.ds(ff + lo, size)
            g = acc[e, :, a] + dot(z[e], ring[slot, :, a])
            u = acc[e, :, b] + dot(z[e], ring[slot, :, b])
            hstage[lax.rem(e, 2), :, a] = (jax.nn.silu(g) * u).astype(BF16)
        h_out(e).start()
        return 0

    lax.fori_loop(0, experts, final_step, 0)
    cw_out(last - 2).wait()
    cws[last % 2] = weigh(last)
    cw_out(last).start()

    for s in (last - 1, last):
        cw_out(s).wait()
    for e in (experts - 2, experts - 1):
        h_out(e).wait()
    hs_out.wait()
    for s in range(1, n):
        tell(s).wait_send()

    def drain(k, _):
        for kind in range(len(kinds)):
            move(kind, k).wait_send()
        return 0

    lax.fori_loop(0, pieces, drain, 0)


def reduce_kernel(
    n, h_hbm, cw_hbm, hs_hbm, wd_hbm, sd_hbm,
    y_hbm,
    h, cw, hs, out, ynear, yown, pair_out, far_out, near_out, ystage, pair_in, far_in, near_in, ring, sring,
    load_sem, pair_send, pair_recv, far_send, far_recv, near_send, near_recv, w_sem, s_sem, y_sem,
):
    me, at = neighbours(n)
    experts, rows_e, ff = h_hbm.shape
    tokens, depth = y_hbm.shape
    chunks = depth // OUT
    pad = rows_e // n
    half = tokens // 2
    total = chunks * experts

    def columns(c):
        return pl.ds(pl.multiple_of(c * OUT, OUT), OUT)

    def load_h(e):
        return pltpu.make_async_copy(h_hbm.at[e], h.at[e], load_sem.at[e])

    load_cw = pltpu.make_async_copy(cw_hbm, cw, load_sem.at[experts])
    load_hs = pltpu.make_async_copy(hs_hbm, hs, load_sem.at[experts + 1])

    def fetch(i):
        slot = lax.rem(i, DOWN_RING)
        return pltpu.make_async_copy(
            wd_hbm.at[lax.rem(i, experts), :, columns(i // experts)], ring.at[slot], w_sem.at[slot]
        )

    def fetch_shared(c):
        slot = lax.rem(c, 2)
        return pltpu.make_async_copy(sd_hbm.at[:, columns(c)], sring.at[slot], s_sem.at[slot])

    other = (FAR_X, RIGHT_X, LEFT_X, PARTNER)
    I_FAR, I_RIGHT, I_LEFT, I_OWN = range(4)

    def pair(i, c):
        return pltpu.make_async_remote_copy(
            src_ref=pair_out.at[lax.rem(c, 2), i],
            dst_ref=pair_in.at[c, i],
            send_sem=pair_send.at[i, lax.rem(c, 2)],
            recv_sem=pair_recv.at[i, c],
            device_id={"ep": at(PARTNER)},
            device_id_type=MESH,
        )

    def far(side, c):
        return pltpu.make_async_remote_copy(
            src_ref=far_out.at[lax.rem(c, 2), pl.ds(side * half, half), :],
            dst_ref=far_in.at[c, side],
            send_sem=far_send.at[side, lax.rem(c, 2)],
            recv_sem=far_recv.at[side, c],
            device_id={"ep": at((RIGHT, LEFT)[side])},
            device_id_type=MESH,
        )

    def near(side, c):
        return pltpu.make_async_remote_copy(
            src_ref=near_out.at[lax.rem(c, 2), side],
            dst_ref=near_in.at[c, side],
            send_sem=near_send.at[side, lax.rem(c, 2)],
            recv_sem=near_recv.at[side, c],
            device_id={"ep": at((RIGHT, LEFT)[side])},
            device_id_type=MESH,
        )

    def result(c):
        slot = lax.rem(c, 2)
        return pltpu.make_async_copy(ystage.at[slot], y_hbm.at[:, columns(c)], y_sem.at[slot])

    load_h(0).start()
    for i in range(DOWN_RING - 1):
        fetch(i).start()
        if i + 1 < experts:
            load_h(i + 1).start()
    for e in range(DOWN_RING, experts):
        load_h(e).start()
    load_cw.start()
    load_hs.start()
    fetch_shared(0).start()
    meet([at(s) for s in (PARTNER, RIGHT, LEFT)])

    def make(c):
        def step(e, _):
            i = c * experts + e

            @pl.when(i + DOWN_RING - 1 < total)
            def _():
                fetch(i + DOWN_RING - 1).start()

            fetch(i).wait()

            @pl.when(c == 0)
            def _():
                load_h(e).wait()

            got = dot(h[e], ring[lax.rem(i, DOWN_RING)]).astype(BF16)
            at_row = pl.ds(pl.multiple_of(e * pad, pad), pad)
            for s in range(n):
                out[s, at_row, :] = got[s * pad : (s + 1) * pad]
            return 0

        lax.fori_loop(0, experts, step, 0)

        @pl.when(c == 0)
        def _():
            load_cw.wait()
            load_hs.wait()

        @pl.when(c >= 2)
        def _():
            for i in range(4):
                pair(i, c - 2).wait_send()
            for side in range(2):
                far(side, c - 2).wait_send()

        @pl.when(c + 1 < chunks)
        def _():
            fetch_shared(c + 1).start()

        for i in range(4):
            s = other[i]
            pair_out[lax.rem(c, 2), i] = dot(cw[s], out[s]).astype(BF16)
            pair(i, c).start()
        ynear[lax.rem(c, 2), 0] = dot(cw[RIGHT], out[RIGHT])
        ynear[lax.rem(c, 2), 1] = dot(cw[LEFT], out[LEFT])
        fetch_shared(c).wait()
        yown[lax.rem(c, 4)] = dot(hs[...], sring[lax.rem(c, 2)]) + dot(cw[OWN], out[OWN])
        mine = dot(cw[FAR], out[FAR])
        pair(I_FAR, c).wait_recv()
        far_out[lax.rem(c, 2)] = (mine + pair_in[c, I_FAR].astype(F32)).astype(BF16)
        far(0, c).start()
        far(1, c).start()

    def pass_on(c):
        slot = lax.rem(c, 2)

        @pl.when(c >= 2)
        def _():
            for side in range(2):
                near(side, c - 2).wait_send()

        for side, i in ((0, I_RIGHT), (1, I_LEFT)):
            pair(i, c).wait_recv()
            far(side, c).wait_recv()
            both, alone = pl.ds(side * half, half), pl.ds((1 - side) * half, half)
            near_out[slot, side, alone] = (ynear[slot, side, alone] + pair_in[c, i, alone].astype(F32)).astype(BF16)
            near_out[slot, side, both] = (
                ynear[slot, side, both] + pair_in[c, i, both].astype(F32) + far_in[c, side].astype(F32)
            ).astype(BF16)
            near(side, c).start()

    def finish(c):
        slot = lax.rem(c, 2)

        @pl.when(c >= 2)
        def _():
            result(c - 2).wait()

        pair(I_OWN, c).wait_recv()
        near(0, c).wait_recv()
        near(1, c).wait_recv()
        ystage[slot] = (
            yown[lax.rem(c, 4)]
            + pair_in[c, I_OWN].astype(F32)
            + near_in[c, 0].astype(F32)
            + near_in[c, 1].astype(F32)
        ).astype(BF16)
        result(c).start()

    def chunk(c, _):
        @pl.when(c < chunks)
        def _():
            make(c)

        @pl.when((c >= 1) & (c <= chunks))
        def _():
            pass_on(c - 1)

        @pl.when(c >= 3)
        def _():
            finish(c - 3)

        return 0

    lax.fori_loop(0, chunks + 3, chunk, 0)
    for c in (chunks - 2, chunks - 1):
        result(c).wait()
        for i in range(4):
            pair(i, c).wait_send()
        for side in range(2):
            far(side, c).wait_send()
            near(side, c).wait_send()


def solution(mesh):
    n = mesh.shape["ep"]
    assert n == 8

    def body(x, expert, slot, gate, w_gate, w_up, w_down, s_gate, s_up, s_down):
        x, expert, slot, gate = x[0, 0], expert[0, 0], slot[0, 0], gate[0, 0]
        (tokens, depth), top = x.shape, expert.shape[1]
        experts, _, ff = w_gate.shape
        shared = s_gate.shape[1]
        slots = 5 * tokens * top // (4 * experts * n)
        pad = -(-slots // 16) * 16
        rows = experts * pad
        pieces, chunks, half = depth // PIECE, depth // OUT, tokens // 2
        top_k = 8
        assert top <= top_k and shared == 2 * ff and rows % 128 == 0
        place = jnp.where(slot < slots, expert * pad + slot, -1).astype(F32)
        grow = ((0, 0), (0, top_k - top))
        info = jnp.concatenate([jnp.pad(place, grow, constant_values=-1), jnp.pad(gate, grow)], axis=1).T

        dma = pltpu.SemaphoreType.DMA
        h, cw, hs = pl.pallas_call(
            functools.partial(gather_kernel, n, slots),
            out_shape=(
                jax.ShapeDtypeStruct((experts, n * pad, ff), BF16),
                jax.ShapeDtypeStruct((n, tokens, rows), BF16),
                jax.ShapeDtypeStruct((tokens, shared), BF16),
            ),
            in_specs=[ANY] * 6,
            out_specs=(ANY,) * 3,
            scratch_shapes=[
                pltpu.VMEM((pieces, n, tokens, PIECE), BF16),
                pltpu.VMEM((n, 2 * top_k, tokens), F32),
                pltpu.VMEM((experts, n * pad, 2 * ff), F32),
                pltpu.VMEM((experts, n * pad, PIECE), BF16),
                pltpu.VMEM((n, rows, tokens), BF16),
                pltpu.VMEM((2, tokens, rows), BF16),
                pltpu.VMEM((tokens, shared), BF16),
                pltpu.VMEM((2, n * pad, ff), BF16),
                pltpu.VMEM((RING, PIECE, 2 * ff), BF16),
                dma((pieces + 1,)),
                dma((n,)),
                dma((n,)),
                dma((8, pieces)),
                dma((8, pieces)),
                dma((RING, 2)),
                dma,
                dma((2,)),
                dma((2,)),
            ],
            compiler_params=pltpu.CompilerParams(
                collective_id=0, has_side_effects=True, vmem_limit_bytes=VMEM_LIMIT
            ),
            name="gather",
        )(x, info, w_gate, w_up, s_gate, s_up)
        y = pl.pallas_call(
            functools.partial(reduce_kernel, n),
            out_shape=jax.ShapeDtypeStruct((tokens, depth), BF16),
            in_specs=[ANY] * 5,
            out_specs=ANY,
            scratch_shapes=[
                pltpu.VMEM((experts, n * pad, ff), BF16),
                pltpu.VMEM((n, tokens, rows), BF16),
                pltpu.VMEM((tokens, shared), BF16),
                pltpu.VMEM((n, rows, OUT), BF16),
                pltpu.VMEM((2, 2, tokens, OUT), F32),
                pltpu.VMEM((4, tokens, OUT), F32),
                pltpu.VMEM((2, 4, tokens, OUT), BF16),
                pltpu.VMEM((2, tokens, OUT), BF16),
                pltpu.VMEM((2, 2, tokens, OUT), BF16),
                pltpu.VMEM((2, tokens, OUT), BF16),
                pltpu.VMEM((chunks, 4, tokens, OUT), BF16),
                pltpu.VMEM((chunks, 2, half, OUT), BF16),
                pltpu.VMEM((chunks, 2, tokens, OUT), BF16),
                pltpu.VMEM((DOWN_RING, ff, OUT), BF16),
                pltpu.VMEM((2, shared, OUT), BF16),
                dma((experts + 2,)),
                dma((4, 2)),
                dma((4, chunks)),
                dma((2, 2)),
                dma((2, chunks)),
                dma((2, 2)),
                dma((2, chunks)),
                dma((DOWN_RING,)),
                dma((2,)),
                dma((2,)),
            ],
            compiler_params=pltpu.CompilerParams(
                collective_id=1, has_side_effects=True, vmem_limit_bytes=VMEM_LIMIT
            ),
            name="reduce",
        )(h, cw, hs, w_down, s_down)
        return y[None, None]

    token, part, whole = P("dp", "ep"), P("ep"), P()
    return jax.shard_map(
        body,
        mesh=mesh,
        in_specs=(token,) * 4 + (part,) * 3 + (whole,) * 3,
        out_specs=token,
        check_vma=False,
    )
```

time: 451 us -> 191 us (0.42); the launches traced: 442 us -> 191 us
  matrix products: 220 us -> 0 us
  Pallas kernels: 0 us -> 186 us
  local copies, waits for them, and re-layouts: 78.3 us -> 3.43 us
  waiting for transfers between devices: 59.8 us -> 0 us
  blocking collectives: 46.2 us -> 0 us
  other arithmetic: 24.4 us -> 1.34 us
  between operations: 13.9 us -> 0.02 us
    dot_general x7 -> x0, matrix products: 220 us -> none  [dot(): return jnp.einsum(form, a, b, preferred_element_type=F32)]
    pallas_call x0 -> x2, Pallas kernels: none -> 186 us  [the longest x1 105 us: body(): pl.pallas_call(functools.partial(gather_kernel, n, slots), out_shape=(jax...]
    reduce_scatter x1 -> x0, waiting for transfers between devices: 59 us -> none  [body(): y = lax.psum_scatter(y, 'ep')]
    all_gather x2 -> x0, blocking collectives: 46.2 us -> none  [the longest x1 24.6 us: body(): places = lax.all_gather(place, 'ep')]
    convert_element_type x2 -> x0, local copies, waits for them, and re-layouts: 42 us -> none  [the longest x1 25.2 us: body(): out = dot('erf,efd->erd', h.astype(BF16), w_down).astype(BF16)]
    transpose x2 -> x0, local copies, waits for them, and re-layouts: 34.9 us -> none  [the longest x1 17.5 us: body(): z.reshape(z.shape[0], mine, slots, -1).swapaxes(0, 1)]
    reduce_sum x1 -> x0, other arithmetic: 16 us -> none  [body(): combine = jnp.sum(jnp.where(hot, gates[..., None], 0), axis=2).astype(BF16)]
    reduce_or x1 -> x0, other arithmetic: 7.64 us -> none  [body(): dispatch = jnp.any(hot, axis=2).astype(BF16)]
  transfers between devices with their start and end apart: 2 -> 0, of which waited for: 1 -> 0; matrix products, arithmetic and copies ran while one was open for 8% -> 0% of each run, Pallas kernels for 0% -> 0%
where the time goes in v2:
time: 191 us
  Pallas kernels  186 us (97%)
  local copies, waits for them, and re-layouts  3.43 us (2%)
    pallas_call x1, Pallas kernels, body(): pl.pallas_call(functools.partial(gather_kernel, n, slots), out_shape=(jax...  105 us
    pallas_call x1, Pallas kernels, body(): pl.pallas_call(functools.partial(reduce_kernel, n), out_shape=jax.ShapeDt...  81.2 us

profile of v2, /device:TPU:112, one launch (start us, length us, event | category | flops | bytes accessed | tf_op | source)
XLA Modules:
  0.0 190.9 jit_solution(9879378288712871435)
XLA Ops:
  0.0 0.7 fusion.3
  0.7 0.7 copy.29
  1.4 0.6 fusion.info_hbm
  2.0 104.9 %gather.1 = (bf16[8,384,1408]{2,1,0:T(8,128)(2,1)}, bf16[8,384,384]{2,1,0:T(8,128)(2,1)}, bf16[384,2816]{1,0:T(8,128)(2,1)}) custom-call(bf16[384,2048]{1,0:T(8,128)(2,1)} %bitcast.10, f32[16,384]{1,0:T(8,128)} %fusion.info_hbm, bf16[8,2048,1408]{2,1,0:T(8,128)(2,1)} %wg_hbm.1, bf16[8,2048,1408]{2,1,0:T(8,128)(2,1)} %wu_hbm.1, bf16[2048,2816]{1,0:T(8,128)(2,1)} %sg_hbm.1, ...), custom_call_target="tpu_custom_call" | custom-call | tf_op jit(solution)/shard_map/gather/pallas_call | solution.py:518
  107.0 81.2 %reduce.1 = bf16[384,2048]{1,0:T(8,128)(2,1)} custom-call(bf16[8,384,1408]{2,1,0:T(8,128)(2,1)} %get-tuple-element.8.h_hbm, bf16[8,384,384]{2,1,0:T(8,128)(2,1)} %get-tuple-element.9.cw_hbm, bf16[384,2816]{1,0:T(8,128)(2,1)} %get-tuple-element.10.hs_hbm, bf16[8,1408,2048]{2,1,0:T(8,128)(2,1)} %wd_hbm.1, bf16[2816,2048]{1,0:T(8,128)(2,1)} %sd_hbm.1), custom_call_target="tpu_custom_call" | custom-call | tf_op jit(solution)/shard_map/reduce/pallas_call | solution.py:552
  188.1 2.7 %copy.31 = bf16[1,1,384,2048]{3,2,1,0:T(8,128)(2,1)} copy(bf16[1,1,384,2048]{3,2,1,0:T(8,128)(2,1)} %bitcast.9) | data formatting | bytes 3145728

commit v3 on v2

--- a/solution.py
+++ b/solution.py
@@ -13,9 +13,13 @@
 VMEM_LIMIT = 67_043_328
 
 PIECE = 256
+UNIT = 512
 OUT = 256
-RING = 4
-DOWN_RING = 6
+AHEAD = 2
+RING = 3
+SPLIT = 5
+SLAB = 512
+DOWN_RING = 8
 
 OWN, PARTNER, RIGHT, RIGHT_X, FAR, FAR_X, LEFT, LEFT_X = range(8)
 
@@ -46,8 +50,8 @@
 def gather_kernel(
     n, slots, x_hbm, info_hbm, wg_hbm, wu_hbm, sg_hbm, su_hbm,
     h_hbm, cw_hbm, hs_hbm,
-    xg, info, acc, z, hot, cws, hs, hstage, ring,
-    load_sem, info_send, info_recv, send_sem, recv_sem, w_sem, out_sem, cw_sem, h_sem,
+    xg, info, acc, z, hot, cws, hstage, ring,
+    load_sem, info_send, info_recv, send_sem, recv_sem, w_sem, cw_sem, h_sem,
 ):
     me, at = neighbours(n)
     tokens, depth = x_hbm.shape
@@ -56,8 +60,9 @@
     pad = z.shape[1] // n
     rows = experts * pad
     half = tokens // 2
-    shared_steps = 2 * pieces
-    total = shared_steps + pieces * experts
+    units, per = depth // UNIT, UNIT // PIECE
+    shared_steps = 2 * units
+    total = shared_steps + units * experts
 
     top, bottom, every = pl.ds(0, half), pl.ds(half, half), pl.ds(0, tokens)
     kinds = (
@@ -103,24 +108,24 @@
 
     def fetch_shared(which, k, slot):
         w = (sg_hbm, su_hbm)[which]
-        return pltpu.make_async_copy(w.at[pl.ds(k * PIECE, PIECE), :], ring.at[slot], w_sem.at[slot, 0])
+        return pltpu.make_async_copy(w.at[pl.ds(k * UNIT, UNIT), :], ring.at[slot], w_sem.at[slot, 0])
 
     def fetch_routed(k, e, slot):
         return (
-            pltpu.make_async_copy(wg_hbm.at[e, pl.ds(k * PIECE, PIECE), :], ring.at[slot, :, pl.ds(0, ff)], w_sem.at[slot, 0]),
-            pltpu.make_async_copy(wu_hbm.at[e, pl.ds(k * PIECE, PIECE), :], ring.at[slot, :, pl.ds(ff, ff)], w_sem.at[slot, 1]),
+            pltpu.make_async_copy(wg_hbm.at[e, pl.ds(k * UNIT, UNIT), :], ring.at[slot, :, pl.ds(0, ff)], w_sem.at[slot, 0]),
+            pltpu.make_async_copy(wu_hbm.at[e, pl.ds(k * UNIT, UNIT), :], ring.at[slot, :, pl.ds(ff, ff)], w_sem.at[slot, 1]),
         )
 
     def start(i):
         slot = lax.rem(i, RING)
 
-        @pl.when(i < pieces)
+        @pl.when(i < units)
         def _():
             fetch_shared(0, i, slot).start()
 
-        @pl.when((i >= pieces) & (i < shared_steps))
-        def _():
-            fetch_shared(1, i - pieces, slot).start()
+        @pl.when((i >= units) & (i < shared_steps))
+        def _():
+            fetch_shared(1, i - units, slot).start()
 
         @pl.when((i >= shared_steps) & (i < total))
         def _():
@@ -143,7 +148,7 @@
     meet([at(s) for s in range(1, n)])
     for k in range(pieces):
         load_x(k).wait()
-        if k < 2:
+        if k < AHEAD:
             move(1, k).start()
             move(2, k).start()
         move(0, k).start()
@@ -152,16 +157,6 @@
             for s in range(1, n):
                 tell(s).start()
 
-    def shared_step(i, _):
-        slot = lax.rem(i, RING)
-        start(i + RING - 1)
-        fetch_shared(0, 0, slot).wait()
-        k = lax.rem(i, pieces)
-        accumulate(i // pieces, xg[k, OWN], slot, k == 0)
-        return 0
-
-    lax.fori_loop(0, shared_steps, shared_step, 0)
-
     def near(k):
         move(1, k).wait_recv()
         move(2, k).wait_recv()
@@ -170,91 +165,148 @@
         move(5, k).start()
         move(6, k).start()
 
-        @pl.when(k + 2 < pieces)
-        def _():
-            move(1, k + 2).start()
-            move(2, k + 2).start()
-
-    near(0)
-
-    width = ring.shape[2]
-    for lo in range(0, width, 256):
-        cut = pl.ds(lo, min(256, width - lo))
-        hs[:, cut] = (jax.nn.silu(acc[0, :, cut]) * acc[1, :, cut]).astype(BF16)
-    hs_out = pltpu.make_async_copy(hs, hs_hbm, out_sem)
-    hs_out.start()
-
-    base = (me * rows).astype(F32)
-    row = lax.broadcasted_iota(jnp.int32, (rows, tokens), 0).astype(F32) + base
+        @pl.when(k + AHEAD < pieces)
+        def _():
+            move(1, k + AHEAD).start()
+            move(2, k + AHEAD).start()
+
+    def far(k):
+        move(3, k).wait_recv()
+        move(4, k).wait_recv()
+        move(7, k).start()
+
+    def shared_step(i, _):
+        slot = lax.rem(i, RING)
+        start(i + RING - 1)
+        fetch_shared(0, 0, slot).wait()
+        u = lax.rem(i, units)
+        mine = jnp.concatenate([xg[u * per + p, OWN] for p in range(per)], axis=1)
+        accumulate(i // units, mine, slot, u == 0)
+
+        @pl.when(i == shared_steps - 3)
+        def _():
+            near(0)
+
+        return 0
+
+    lax.fori_loop(0, shared_steps, shared_step, 0)
+
+    def hs_out(i):
+        return pltpu.make_async_copy(hstage.at[i], hs_hbm.at[i], h_sem.at[i])
+
+    for i in range(2):
+        for lo in range(0, ff, 256):
+            size = min(256, ff - lo)
+            cut = pl.ds(i * ff + lo, size)
+            hstage[i, :, pl.ds(lo, size)] = (jax.nn.silu(acc[0, :, cut]) * acc[1, :, cut]).astype(BF16)
+        hs_out(i).start()
+
     top_k = info.shape[1] // 2
+    first_row = (me * experts + lax.broadcasted_iota(jnp.int32, (experts, tokens), 0)) * pad
+    first_row = first_row.astype(F32)
+    in_slot = lax.broadcasted_iota(jnp.int32, (pad, tokens), 0).astype(F32)
+
+    def table(s, weighted):
+        at_slot = jnp.full((experts, tokens), -1.0, F32)
+        weight = jnp.zeros((experts, tokens), F32)
+        for j in range(top_k):
+            here = info[s, pl.ds(j, 1), :] - first_row
+            hit = (here >= 0) & (here < pad)
+            at_slot = jnp.where(hit, here, at_slot)
+            if weighted:
+                weight = jnp.where(hit, info[s, pl.ds(top_k + j, 1), :], weight)
+        return at_slot, weight
 
     for s in range(n):
         if s:
             tell(opposite(s)).wait_recv()
-        found = jnp.zeros((rows, tokens), F32)
-        for j in range(top_k):
-            found = jnp.where(row == info[s, pl.ds(j, 1), :], 1.0, found)
-        hot[s] = found.astype(BF16)
+        at_slot, _ = table(s, False)
+        for e in range(experts):
+            hit = in_slot == at_slot[e : e + 1]
+            hot[s, pl.ds(e * pad, pad), :] = jnp.where(hit, 1.0, 0.0).astype(BF16)
+
+    near(1)
 
     def weigh(s):
-        found = jnp.zeros((rows, tokens), F32)
-        for j in range(top_k):
-            found = jnp.where(row == info[s, pl.ds(j, 1), :], info[s, pl.ds(top_k + j, 1), :], found)
-        return found.T.astype(BF16)
+        at_slot, weight = table(s, True)
+        found = [jnp.where(in_slot == at_slot[e : e + 1], weight[e : e + 1], 0.0) for e in range(experts)]
+        return jnp.concatenate(found, axis=0).T.astype(BF16)
 
     def cw_out(s):
         return pltpu.make_async_copy(cws.at[lax.rem(s, 2)], cw_hbm.at[s], cw_sem.at[lax.rem(s, 2)])
 
-    def dispatch(k):
+    def place(k, p, sources):
+        for s in sources:
+            got = dot(hot[s], xg[k, s]).astype(BF16)
+            for e in range(experts):
+                z[e, s * pad : (s + 1) * pad, pl.ds(p * PIECE, PIECE)] = got[e * pad : (e + 1) * pad]
+
+    def place_near(k, p):
         move(0, k).wait_recv()
         move(5, k).wait_recv()
         move(6, k).wait_recv()
-
-        def place(s):
-            got = dot(hot[s], xg[k, s]).astype(BF16)
-            for e in range(experts):
-                z[e, s * pad : (s + 1) * pad, :] = got[e * pad : (e + 1) * pad]
-
-        for s in (OWN, PARTNER, RIGHT, LEFT, RIGHT_X, LEFT_X):
-            place(s)
-        move(3, k).wait_recv()
-        move(4, k).wait_recv()
-        move(7, k).start()
-        place(FAR)
+        place(k, p, (OWN, PARTNER, RIGHT, LEFT, RIGHT_X, LEFT_X))
+
+    def place_far(k, p):
+        place(k, p, (FAR,))
         move(7, k).wait_recv()
-        place(FAR_X)
-
-    def piece(k, _):
-        dispatch(k)
-
+        place(k, p, (FAR_X,))
+
+    def weigh_out(s):
+        @pl.when(s >= 2)
+        def _():
+            cw_out(s - 2).wait()
+
+        cws[lax.rem(s, 2)] = weigh(s)
+        cw_out(s).start()
+
+    assert per == 2
+
+    def weigh_all(s, _):
+        weigh_out(s)
+        return 0
+
+    lax.fori_loop(0, n, weigh_all, 0)
+    far(0)
+    place_near(0, 0)
+    place_near(1, 1)
+    near(2)
+    far(1)
+    place_far(0, 0)
+    place_far(1, 1)
+
+    def unit(u, _):
         def step(e, _):
-            i = shared_steps + k * experts + e
+            i = shared_steps + u * experts + e
             slot = lax.rem(i, RING)
             start(i + RING - 1)
             for c in fetch_routed(0, 0, slot):
                 c.wait()
-            accumulate(e, z[e], slot, k == 0)
-
-            @pl.when(e == experts // 2 - 1)
+            accumulate(e, z[e], slot, u == 0)
+
+            @pl.when((e == 1) | ((e == 6) & (2 * u + 4 < pieces)))
             def _():
-                near(k + 1)
+                near(2 * u + 3 + e // 6)
+
+            @pl.when(e == 4)
+            def _():
+                far(2 * u + 2)
 
             return 0
 
         lax.fori_loop(0, experts, step, 0)
-
-        @pl.when(k >= 2)
-        def _():
-            cw_out(k - 2).wait()
-
-        cws[lax.rem(k, 2)] = weigh(k)
-        cw_out(k).start()
+        k = 2 * u + 2
+        place_near(k, 0)
+        place_far(k, 0)
+        far(k + 1)
+        place_near(k + 1, 1)
+        place_far(k + 1, 1)
         return 0
 
-    assert pieces == n
-    lax.fori_loop(0, pieces - 1, piece, 0)
-    last = pieces - 1
-    dispatch(last)
+    lax.fori_loop(0, units - 1, unit, 0)
+    for i in range(2):
+        hs_out(i).wait()
+    last = units - 1
 
     def h_out(e):
         return pltpu.make_async_copy(hstage.at[lax.rem(e, 2)], h_hbm.at[e], h_sem.at[lax.rem(e, 2)])
@@ -280,15 +332,11 @@
         return 0
 
     lax.fori_loop(0, experts, final_step, 0)
-    cw_out(last - 2).wait()
-    cws[last % 2] = weigh(last)
-    cw_out(last).start()
-
-    for s in (last - 1, last):
+
+    for s in (n - 2, n - 1):
         cw_out(s).wait()
     for e in (experts - 2, experts - 1):
         h_out(e).wait()
-    hs_out.wait()
     for s in range(1, n):
         tell(s).wait_send()
 
@@ -303,7 +351,7 @@
 def reduce_kernel(
     n, h_hbm, cw_hbm, hs_hbm, wd_hbm, sd_hbm,
     y_hbm,
-    h, cw, hs, out, ynear, yown, pair_out, far_out, near_out, ystage, pair_in, far_in, near_in, ring, sring,
+    h, cw, hs, out, yshared, ynear, yown, pair_out, far_out, near_out, ystage, pair_in, far_in, near_in, ring, sring,
     load_sem, pair_send, pair_recv, far_send, far_recv, near_send, near_recv, w_sem, s_sem, y_sem,
 ):
     me, at = neighbours(n)
@@ -312,7 +360,9 @@
     chunks = depth // OUT
     pad = rows_e // n
     half = tokens // 2
-    total = chunks * experts
+    per = SLAB // OUT
+    slabs = chunks // per
+    total = slabs * experts
 
     def columns(c):
         return pl.ds(pl.multiple_of(c * OUT, OUT), OUT)
@@ -322,16 +372,19 @@
 
     load_cw = pltpu.make_async_copy(cw_hbm, cw, load_sem.at[experts])
     load_hs = pltpu.make_async_copy(hs_hbm, hs, load_sem.at[experts + 1])
+
+    def slab(q):
+        return pl.ds(pl.multiple_of(q * SLAB, SLAB), SLAB)
 
     def fetch(i):
         slot = lax.rem(i, DOWN_RING)
         return pltpu.make_async_copy(
-            wd_hbm.at[lax.rem(i, experts), :, columns(i // experts)], ring.at[slot], w_sem.at[slot]
+            wd_hbm.at[lax.rem(i, experts), :, slab(i // experts)], ring.at[slot], w_sem.at[slot]
         )
 
-    def fetch_shared(c):
-        slot = lax.rem(c, 2)
-        return pltpu.make_async_copy(sd_hbm.at[:, columns(c)], sring.at[slot], s_sem.at[slot])
+    def fetch_shared(q):
+        slot = lax.rem(q, 2)
+        return pltpu.make_async_copy(sd_hbm.at[:, slab(q)], sring.at[slot], s_sem.at[slot])
 
     other = (FAR_X, RIGHT_X, LEFT_X, PARTNER)
     I_FAR, I_RIGHT, I_LEFT, I_OWN = range(4)
@@ -371,68 +424,79 @@
         return pltpu.make_async_copy(ystage.at[slot], y_hbm.at[:, columns(c)], y_sem.at[slot])
 
     load_h(0).start()
-    for i in range(DOWN_RING - 1):
+    for i in range(experts):
         fetch(i).start()
         if i + 1 < experts:
             load_h(i + 1).start()
-    for e in range(DOWN_RING, experts):
-        load_h(e).start()
     load_cw.start()
     load_hs.start()
     fetch_shared(0).start()
+    for i in range(experts, DOWN_RING):
+        fetch(i).start()
+    fetch_shared(1).start()
     meet([at(s) for s in (PARTNER, RIGHT, LEFT)])
 
+    def down(q, begin, end, first=False):
+        side = lax.rem(q, 2)
+
+        def step(e, _):
+            i = q * experts + e
+            slot = lax.rem(i, DOWN_RING)
+            fetch(i).wait()
+            if first:
+                load_h(e).wait()
+            got = dot(h[e], ring[slot]).astype(BF16)
+            at_row = pl.ds(pl.multiple_of(e * pad, pad), pad)
+            for p in range(per):
+                for s in range(n):
+                    out[side, p, s, at_row, :] = got[s * pad : (s + 1) * pad, p * OUT : (p + 1) * OUT]
+
+            @pl.when(i + DOWN_RING < total)
+            def _():
+                fetch(i + DOWN_RING).start()
+
+            return 0
+
+        lax.fori_loop(begin, min(end, experts), step, 0)
+        if end > experts:
+            fetch_shared(q).wait()
+            if first:
+                load_hs.wait()
+            got = dot(jnp.concatenate([hs[0], hs[1]], axis=1), sring[side])
+            for p in range(per):
+                yshared[side, p] = got[:, p * OUT : (p + 1) * OUT]
+
+            @pl.when(q + 2 < slabs)
+            def _():
+                fetch_shared(q + 2).start()
+
     def make(c):
-        def step(e, _):
-            i = c * experts + e
-
-            @pl.when(i + DOWN_RING - 1 < total)
-            def _():
-                fetch(i + DOWN_RING - 1).start()
-
-            fetch(i).wait()
-
-            @pl.when(c == 0)
-            def _():
-                load_h(e).wait()
-
-            got = dot(h[e], ring[lax.rem(i, DOWN_RING)]).astype(BF16)
-            at_row = pl.ds(pl.multiple_of(e * pad, pad), pad)
-            for s in range(n):
-                out[s, at_row, :] = got[s * pad : (s + 1) * pad]
-            return 0
-
-        lax.fori_loop(0, experts, step, 0)
-
-        @pl.when(c == 0)
-        def _():
-            load_cw.wait()
-            load_hs.wait()
+        side, p = lax.rem(c // per, 2), lax.rem(c, per)
 
         @pl.when(c >= 2)
         def _():
             for i in range(4):
                 pair(i, c - 2).wait_send()
-            for side in range(2):
-                far(side, c - 2).wait_send()
-
-        @pl.when(c + 1 < chunks)
-        def _():
-            fetch_shared(c + 1).start()
+            for way in range(2):
+                far(way, c - 2).wait_send()
 
         for i in range(4):
             s = other[i]
-            pair_out[lax.rem(c, 2), i] = dot(cw[s], out[s]).astype(BF16)
+            pair_out[lax.rem(c, 2), i] = dot(cw[s], out[side, p, s]).astype(BF16)
             pair(i, c).start()
-        ynear[lax.rem(c, 2), 0] = dot(cw[RIGHT], out[RIGHT])
-        ynear[lax.rem(c, 2), 1] = dot(cw[LEFT], out[LEFT])
-        fetch_shared(c).wait()
-        yown[lax.rem(c, 4)] = dot(hs[...], sring[lax.rem(c, 2)]) + dot(cw[OWN], out[OWN])
-        mine = dot(cw[FAR], out[FAR])
+        ynear[lax.rem(c, 2), 0] = dot(cw[RIGHT], out[side, p, RIGHT])
+        ynear[lax.rem(c, 2), 1] = dot(cw[LEFT], out[side, p, LEFT])
+        yown[lax.rem(c, 4)] = yshared[side, p] + dot(cw[OWN], out[side, p, OWN])
+        mine = dot(cw[FAR], out[side, p, FAR])
         pair(I_FAR, c).wait_recv()
         far_out[lax.rem(c, 2)] = (mine + pair_in[c, I_FAR].astype(F32)).astype(BF16)
         far(0, c).start()
         far(1, c).start()
+        for j in range(per):
+
+            @pl.when((p == j) & (c // per + 1 < slabs))
+            def _():
+                down(c // per + 1, (0, SPLIT)[j], (SPLIT, experts + 1)[j])
 
     def pass_on(c):
         slot = lax.rem(c, 2)
@@ -485,6 +549,8 @@
 
         return 0
 
+    down(0, 0, experts + 1, first=True)
+    load_cw.wait()
     lax.fori_loop(0, chunks + 3, chunk, 0)
     for c in (chunks - 2, chunks - 1):
         result(c).wait()
@@ -509,7 +575,7 @@
         rows = experts * pad
         pieces, chunks, half = depth // PIECE, depth // OUT, tokens // 2
         top_k = 8
-        assert top <= top_k and shared == 2 * ff and rows % 128 == 0
+        assert top <= top_k and shared == 2 * ff and n * pad == tokens and rows % 128 == 0
         place = jnp.where(slot < slots, expert * pad + slot, -1).astype(F32)
         grow = ((0, 0), (0, top_k - top))
         info = jnp.concatenate([jnp.pad(place, grow, constant_values=-1), jnp.pad(gate, grow)], axis=1).T
@@ -520,7 +586,7 @@
             out_shape=(
                 jax.ShapeDtypeStruct((experts, n * pad, ff), BF16),
                 jax.ShapeDtypeStruct((n, tokens, rows), BF16),
-                jax.ShapeDtypeStruct((tokens, shared), BF16),
+                jax.ShapeDtypeStruct((2, tokens, ff), BF16),
             ),
             in_specs=[ANY] * 6,
             out_specs=(ANY,) * 3,
@@ -528,19 +594,17 @@
                 pltpu.VMEM((pieces, n, tokens, PIECE), BF16),
                 pltpu.VMEM((n, 2 * top_k, tokens), F32),
                 pltpu.VMEM((experts, n * pad, 2 * ff), F32),
-                pltpu.VMEM((experts, n * pad, PIECE), BF16),
+                pltpu.VMEM((experts, n * pad, UNIT), BF16),
                 pltpu.VMEM((n, rows, tokens), BF16),
                 pltpu.VMEM((2, tokens, rows), BF16),
-                pltpu.VMEM((tokens, shared), BF16),
                 pltpu.VMEM((2, n * pad, ff), BF16),
-                pltpu.VMEM((RING, PIECE, 2 * ff), BF16),
+                pltpu.VMEM((RING, UNIT, 2 * ff), BF16),
                 dma((pieces + 1,)),
                 dma((n,)),
                 dma((n,)),
                 dma((8, pieces)),
                 dma((8, pieces)),
                 dma((RING, 2)),
-                dma,
                 dma((2,)),
                 dma((2,)),
             ],
@@ -557,8 +621,9 @@
             scratch_shapes=[
                 pltpu.VMEM((experts, n * pad, ff), BF16),
                 pltpu.VMEM((n, tokens, rows), BF16),
-                pltpu.VMEM((tokens, shared), BF16),
-                pltpu.VMEM((n, rows, OUT), BF16),
+                pltpu.VMEM((2, tokens, ff), BF16),
+                pltpu.VMEM((2, SLAB // OUT, n, rows, OUT), BF16),
+                pltpu.VMEM((2, SLAB // OUT, tokens, OUT), F32),
                 pltpu.VMEM((2, 2, tokens, OUT), F32),
                 pltpu.VMEM((4, tokens, OUT), F32),
                 pltpu.VMEM((2, 4, tokens, OUT), BF16),
@@ -568,8 +633,8 @@
                 pltpu.VMEM((chunks, 4, tokens, OUT), BF16),
                 pltpu.VMEM((chunks, 2, half, OUT), BF16),
                 pltpu.VMEM((chunks, 2, tokens, OUT), BF16),
-                pltpu.VMEM((DOWN_RING, ff, OUT), BF16),
-                pltpu.VMEM((2, shared, OUT), BF16),
+                pltpu.VMEM((DOWN_RING, ff, SLAB), BF16),
+                pltpu.VMEM((2, shared, SLAB), BF16),
                 dma((experts + 2,)),
                 dma((4, 2)),
                 dma((4, chunks)),

time: 191 us -> 162 us (0.85)
  Pallas kernels: 186 us -> 157 us
    pallas_call x1, Pallas kernels: 105 us -> 82.3 us  [body(): pl.pallas_call(functools.partial(gather_kernel, n, slots), out_shape=(jax...]
    pallas_call x1, Pallas kernels: 81.2 us -> 74.5 us  [body(): pl.pallas_call(functools.partial(reduce_kernel, n), out_shape=jax.ShapeDt...]
where the time goes in v3:
time: 162 us
  Pallas kernels  157 us (97%)
  local copies, waits for them, and re-layouts  3.43 us (2%)
    pallas_call x1, Pallas kernels, body(): pl.pallas_call(functools.partial(gather_kernel, n, slots), out_shape=(jax...  82.3 us
    pallas_call x1, Pallas kernels, body(): pl.pallas_call(functools.partial(reduce_kernel, n), out_shape=jax.ShapeDt...  74.5 us
    unnamed x2, local copies, waits for them, and re-layouts  3.43 us

profile of v3, /device:TPU:112, one launch (start us, length us, event | category | flops | bytes accessed | tf_op | source)
XLA Modules:
  0.0 161.6 jit_solution(9067499933310749009)
XLA Ops:
  0.0 0.7 fusion.3
  0.7 0.7 copy.29
  1.4 0.6 fusion.info_hbm
  2.0 82.3 %gather.1 = (bf16[8,384,1408]{2,1,0:T(8,128)(2,1)}, bf16[8,384,384]{2,1,0:T(8,128)(2,1)}, bf16[2,384,1408]{2,1,0:T(8,128)(2,1)}) custom-call(bf16[384,2048]{1,0:T(8,128)(2,1)} %bitcast.10, f32[16,384]{1,0:T(8,128)} %fusion.info_hbm, bf16[8,2048,1408]{2,1,0:T(8,128)(2,1)} %wg_hbm.1, bf16[8,2048,1408]{2,1,0:T(8,128)(2,1)} %wu_hbm.1, ...), custom_call_target="tpu_custom_call" | custom-call | tf_op jit(solution)/shard_map/gather/pallas_call | solution.py:584
  84.4 74.5 %reduce.1 = bf16[384,2048]{1,0:T(8,128)(2,1)} custom-call(bf16[8,384,1408]{2,1,0:T(8,128)(2,1)} %get-tuple-element.8.h_hbm, bf16[8,384,384]{2,1,0:T(8,128)(2,1)} %get-tuple-element.9.cw_hbm, bf16[2,384,1408]{2,1,0:T(8,128)(2,1)} %get-tuple-element.10.hs_hbm, bf16[8,1408,2048]{2,1,0:T(8,128)(2,1)} %wd_hbm.1, bf16[2816,2048]{1,0:T(8,128)(2,1)} %sd_hbm.1), custom_call_target="tpu_custom_call" | custom-call | tf_op jit(solution)/shard_map/reduce/pallas_call | solution.py:616
  158.9 2.7 %copy.31 = bf16[1,1,384,2048]{3,2,1,0:T(8,128)(2,1)} copy(bf16[1,1,384,2048]{3,2,1,0:T(8,128)(2,1)} %bitcast.9) | data formatting | bytes 3145728

commit v4 on v3

--- a/solution.py
+++ b/solution.py
@@ -15,6 +15,7 @@
 PIECE = 256
 UNIT = 512
 OUT = 256
+CUT = 512
 AHEAD = 2
 RING = 3
 SPLIT = 5
@@ -40,11 +41,14 @@
     return me, at
 
 
-def meet(peers):
+def greet(peers):
     barrier = pltpu.get_barrier_semaphore()
     for peer in peers:
         pl.semaphore_signal(barrier, inc=1, device_id={"ep": peer}, device_id_type=MESH)
-    pl.semaphore_wait(barrier, len(peers))
+
+
+def meet(peers):
+    pl.semaphore_wait(pltpu.get_barrier_semaphore(), len(peers))
 
 
 def gather_kernel(
@@ -135,17 +139,19 @@
 
     def accumulate(a, left, slot, first):
         width = ring.shape[2]
-        for lo in range(0, width, 256):
-            cut = pl.ds(lo, min(256, width - lo))
+        for lo in range(0, width, CUT):
+            cut = pl.ds(lo, min(CUT, width - lo))
             before = jnp.where(first, 0.0, acc[a, :, cut])
             acc[a, :, cut] = before + dot(left, ring[slot, :, cut])
 
+    everyone = [at(s) for s in range(1, n)]
+    greet(everyone)
     for k in range(pieces):
         load_x(k).start()
     load_info.start()
     for i in range(RING - 1):
         fetch_shared(0, i, i).start()
-    meet([at(s) for s in range(1, n)])
+    meet(everyone)
     for k in range(pieces):
         load_x(k).wait()
         if k < AHEAD:
@@ -235,22 +241,25 @@
     def cw_out(s):
         return pltpu.make_async_copy(cws.at[lax.rem(s, 2)], cw_hbm.at[s], cw_sem.at[lax.rem(s, 2)])
 
-    def place(k, p, sources):
+    def place(k, sources):
         for s in sources:
-            got = dot(hot[s], xg[k, s]).astype(BF16)
+            whole = jnp.concatenate([xg[k + p, s] for p in range(per)], axis=1)
+            got = dot(hot[s], whole).astype(BF16)
             for e in range(experts):
-                z[e, s * pad : (s + 1) * pad, pl.ds(p * PIECE, PIECE)] = got[e * pad : (e + 1) * pad]
-
-    def place_near(k, p):
-        move(0, k).wait_recv()
-        move(5, k).wait_recv()
-        move(6, k).wait_recv()
-        place(k, p, (OWN, PARTNER, RIGHT, LEFT, RIGHT_X, LEFT_X))
-
-    def place_far(k, p):
-        place(k, p, (FAR,))
-        move(7, k).wait_recv()
-        place(k, p, (FAR_X,))
+                z[e, s * pad : (s + 1) * pad, :] = got[e * pad : (e + 1) * pad]
+
+    def place_near(k):
+        for p in range(per):
+            move(0, k + p).wait_recv()
+            move(5, k + p).wait_recv()
+            move(6, k + p).wait_recv()
+        place(k, (OWN, PARTNER, RIGHT, LEFT, RIGHT_X, LEFT_X))
+
+    def place_far(k):
+        place(k, (FAR,))
+        for p in range(per):
+            move(7, k + p).wait_recv()
+        place(k, (FAR_X,))
 
     def weigh_out(s):
         @pl.when(s >= 2)
@@ -268,12 +277,10 @@
 
     lax.fori_loop(0, n, weigh_all, 0)
     far(0)
-    place_near(0, 0)
-    place_near(1, 1)
+    place_near(0)
     near(2)
     far(1)
-    place_far(0, 0)
-    place_far(1, 1)
+    place_far(0)
 
     def unit(u, _):
         def step(e, _):
@@ -296,11 +303,9 @@
 
         lax.fori_loop(0, experts, step, 0)
         k = 2 * u + 2
-        place_near(k, 0)
-        place_far(k, 0)
         far(k + 1)
-        place_near(k + 1, 1)
-        place_far(k + 1, 1)
+        place_near(k)
+        place_far(k)
         return 0
 
     lax.fori_loop(0, units - 1, unit, 0)
@@ -361,6 +366,7 @@
     pad = rows_e // n
     half = tokens // 2
     per = SLAB // OUT
+    assert per == 2 and DOWN_RING == experts
     slabs = chunks // per
     total = slabs * experts
 
@@ -423,18 +429,14 @@
         slot = lax.rem(c, 2)
         return pltpu.make_async_copy(ystage.at[slot], y_hbm.at[:, columns(c)], y_sem.at[slot])
 
+    beside = [at(s) for s in (PARTNER, RIGHT, LEFT)]
+    greet(beside)
     load_h(0).start()
     for i in range(experts):
         fetch(i).start()
         if i + 1 < experts:
             load_h(i + 1).start()
     load_cw.start()
-    load_hs.start()
-    fetch_shared(0).start()
-    for i in range(experts, DOWN_RING):
-        fetch(i).start()
-    fetch_shared(1).start()
-    meet([at(s) for s in (PARTNER, RIGHT, LEFT)])
 
     def down(q, begin, end, first=False):
         side = lax.rem(q, 2)
@@ -460,8 +462,6 @@
         lax.fori_loop(begin, min(end, experts), step, 0)
         if end > experts:
             fetch_shared(q).wait()
-            if first:
-                load_hs.wait()
             got = dot(jnp.concatenate([hs[0], hs[1]], axis=1), sring[side])
             for p in range(per):
                 yshared[side, p] = got[:, p * OUT : (p + 1) * OUT]
@@ -486,15 +486,24 @@
             pair(i, c).start()
         ynear[lax.rem(c, 2), 0] = dot(cw[RIGHT], out[side, p, RIGHT])
         ynear[lax.rem(c, 2), 1] = dot(cw[LEFT], out[side, p, LEFT])
-        yown[lax.rem(c, 4)] = yshared[side, p] + dot(cw[OWN], out[side, p, OWN])
+        own = dot(cw[OWN], out[side, p, OWN])
         mine = dot(cw[FAR], out[side, p, FAR])
         pair(I_FAR, c).wait_recv()
         far_out[lax.rem(c, 2)] = (mine + pair_in[c, I_FAR].astype(F32)).astype(BF16)
         far(0, c).start()
         far(1, c).start()
+
+        @pl.when(c == 0)
+        def _():
+            load_hs.wait()
+            down(0, experts, experts + 1)
+
+        yown[lax.rem(c, 4)] = own + yshared[side, p]
+
+    def ahead(c):
         for j in range(per):
 
-            @pl.when((p == j) & (c // per + 1 < slabs))
+            @pl.when((lax.rem(c, per) == j) & (c // per + 1 < slabs))
             def _():
                 down(c // per + 1, (0, SPLIT)[j], (SPLIT, experts + 1)[j])
 
@@ -543,14 +552,22 @@
         def _():
             pass_on(c - 1)
 
+        @pl.when(c < chunks)
+        def _():
+            ahead(c)
+
         @pl.when(c >= 3)
         def _():
             finish(c - 3)
 
         return 0
 
-    down(0, 0, experts + 1, first=True)
+    down(0, 0, experts, first=True)
+    load_hs.start()
+    fetch_shared(0).start()
+    fetch_shared(1).start()
     load_cw.wait()
+    meet(beside)
     lax.fori_loop(0, chunks + 3, chunk, 0)
     for c in (chunks - 2, chunks - 1):
         result(c).wait()

time: 162 us -> 158 us (0.975)
  Pallas kernels: 157 us -> 153 us
    pallas_call x1, Pallas kernels: 82.3 us -> 79.8 us  [body(): pl.pallas_call(functools.partial(gather_kernel, n, slots), out_shape=(jax...]
where the time goes in v4:
time: 158 us
  Pallas kernels  153 us (97%)
  local copies, waits for them, and re-layouts  3.43 us (2%)
    pallas_call x1, Pallas kernels, body(): pl.pallas_call(functools.partial(gather_kernel, n, slots), out_shape=(jax...  79.8 us
    pallas_call x1, Pallas kernels, body(): pl.pallas_call(functools.partial(reduce_kernel, n), out_shape=jax.ShapeDt...  73.4 us
    unnamed x2, local copies, waits for them, and re-layouts  3.43 us

profile of v4, /device:TPU:112, one launch (start us, length us, event | category | flops | bytes accessed | tf_op | source)
XLA Modules:
  0.0 158.0 jit_solution(7802058081068631885)
XLA Ops:
  0.0 0.7 fusion.3
  0.7 0.7 copy.29
  1.4 0.6 fusion.info_hbm
  2.0 79.8 %gather.1 = (bf16[8,384,1408]{2,1,0:T(8,128)(2,1)}, bf16[8,384,384]{2,1,0:T(8,128)(2,1)}, bf16[2,384,1408]{2,1,0:T(8,128)(2,1)}) custom-call(bf16[384,2048]{1,0:T(8,128)(2,1)} %bitcast.10, f32[16,384]{1,0:T(8,128)} %fusion.info_hbm, bf16[8,2048,1408]{2,1,0:T(8,128)(2,1)} %wg_hbm.1, bf16[8,2048,1408]{2,1,0:T(8,128)(2,1)} %wu_hbm.1, ...), custom_call_target="tpu_custom_call" | custom-call | tf_op jit(solution)/shard_map/gather/pallas_call | solution.py:601
  81.8 73.4 %reduce.1 = bf16[384,2048]{1,0:T(8,128)(2,1)} custom-call(bf16[8,384,1408]{2,1,0:T(8,128)(2,1)} %get-tuple-element.8.h_hbm, bf16[8,384,384]{2,1,0:T(8,128)(2,1)} %get-tuple-element.9.cw_hbm, bf16[2,384,1408]{2,1,0:T(8,128)(2,1)} %get-tuple-element.10.hs_hbm, bf16[8,1408,2048]{2,1,0:T(8,128)(2,1)} %wd_hbm.1, bf16[2816,2048]{1,0:T(8,128)(2,1)} %sd_hbm.1), custom_call_target="tpu_custom_call" | custom-call | tf_op jit(solution)/shard_map/reduce/pallas_call | solution.py:633
  155.3 2.7 %copy.31 = bf16[1,1,384,2048]{3,2,1,0:T(8,128)(2,1)} copy(bf16[1,1,384,2048]{3,2,1,0:T(8,128)(2,1)} %bitcast.9) | data formatting | bytes 3145728
